TPU v7x, 8 devices: a whole 2x2x1 slice. The times are simulated.
8 devices in a mesh: seqs: 1 (over z), states: 8 (over y, x, core).
Axes of the slice: x: 2, y: 2, z: 1, core: 2. Of those that a mesh axis runs over, the one named last changes fastest.
Arguments:
- trans_mat: bfloat16 [16384, 16384], P(None, 'states')
- emit_mat: bfloat16 [16384, 10000], P('states')
- init_prob: float32 [16384], P('states')
- tokens: int32 [64, 32], P('seqs')
- lengths: int32 [64], P('seqs')
Outputs:
- output 1: float32 [64], P('seqs')
- output 2: float32 [64, 16384], P('seqs', 'states')
- output 3: float32 [16384, 2048], P(('seqs', 'states'))
All inputs are finite; a program needn't handle non-finite values.
Results may differ from a plain program's by a relative error of at most 0.001.
Values are sent between devices in bfloat16 or wider.
A program may use at most 1 GiB of HBM per device.

v0:
```python
import jax
import jax.numpy as jnp
from jax import lax
from jax.sharding import PartitionSpec as P


def solution(mesh):
    def step_weight(live_mask, emit_now, beta_cur, step_scale):
        scaled = emit_now.astype(jnp.float32) * beta_cur / step_scale[:, None]
        return jnp.where(live_mask[:, None], scaled, 0.0).astype(jnp.bfloat16)

    def local_run(trans_loc, emit_loc, init_loc, tokens_loc, lengths_loc):
        seq_count, step_count = tokens_loc.shape
        block_size = trans_loc.shape[1]
        group_idx = lax.axis_index('states')
        emit_seq = jnp.transpose(jnp.take(emit_loc, tokens_loc.T, axis=1), (1, 2, 0))
        first_mass = init_loc[None, :] * emit_seq[0].astype(jnp.float32)
        first_norm = lax.psum(jnp.sum(first_mass, axis=1), 'states')
        alpha_first = first_mass / first_norm[:, None]
        live_steps = jnp.arange(1, step_count)[:, None] < lengths_loc[None, :]

        def forward_step(alpha_cur, inputs):
            live_mask, emit_now = inputs
            alpha_bf = alpha_cur.astype(jnp.bfloat16)
            alpha_full = lax.all_gather(alpha_bf, 'states', axis=1, tiled=True)
            pred_mass = jnp.dot(alpha_full, trans_loc, preferred_element_type=jnp.float32)
            new_mass = pred_mass * emit_now.astype(jnp.float32)
            norm_sum = lax.psum(jnp.sum(new_mass, axis=1), 'states')
            step_scale = jnp.where(live_mask, norm_sum, 1.0)
            alpha_next = jnp.where(live_mask[:, None], new_mass / norm_sum[:, None], alpha_cur)
            return alpha_next, (alpha_bf, step_scale)

        alpha_last, (alpha_prev, scales) = lax.scan(forward_step, alpha_first, (live_steps, emit_seq[1:]))
        loglik = jnp.log(first_norm) + jnp.sum(jnp.log(scales), axis=0)

        def backward_step(beta_cur, inputs):
            live_mask, emit_now, step_scale = inputs
            weight = step_weight(live_mask, emit_now, beta_cur, step_scale)
            partial_sum = lax.dot_general(weight, trans_loc, (((1,), (1,)), ((), ())), preferred_element_type=jnp.float32)
            beta_prev = lax.psum_scatter(partial_sum, 'states', scatter_dimension=1, tiled=True)
            return beta_prev + jnp.where(live_mask, 0.0, 1.0)[:, None], weight

        beta_one, late_weights = lax.scan(backward_step, jnp.ones((seq_count, block_size), jnp.float32), (live_steps[1:], emit_seq[2:], scales[1:]), reverse=True)
        first_weight = step_weight(live_steps[0], emit_seq[1], beta_one, scales[0])
        pair_sum = jnp.einsum('tbi,tbj->ij', alpha_prev[1:], late_weights, preferred_element_type=jnp.float32)
        pair_sum = pair_sum + lax.dot_general(alpha_prev[0], first_weight, (((0,), (0,)), ((), ())), preferred_element_type=jnp.float32)
        diag_block = lax.dynamic_slice_in_dim(trans_loc, group_idx * block_size, block_size, axis=0)
        counts = diag_block.astype(jnp.float32) * pair_sum
        return loglik, alpha_last, counts

    return jax.shard_map(local_run, mesh=mesh, in_specs=(P(None, 'states'), P('states', None), P('states'), P('seqs', None), P('seqs')), out_specs=(P('seqs'), P('seqs', 'states'), P(('seqs', 'states'), None)), check_vma=False)
```

profile of v0, /device:TPU:0, one launch (start us, length us, event | category | flops | bytes accessed | tf_op | source)
XLA Modules:
  0.0 4648.6 jit_solution(16387322856402332150)
XLA Ops:
  8.0 47.9 %gather_fusion = bf16[2048,2048]{1,0:T(8,128)(2,1)} fusion(bf16[2048,10000]{0,1:T(8,128)(2,1)} %param.10, s32[2048]{0:T(1024)S(1)} %broadcast_clamp_fusion), kind=kCustom, calls=%fused_computation | custom fusion | bytes 16785408 | tf_op jit(solution)/shard_map/jit(_take)/gather | solution.py:16
  99.2 2307.8 %while.31 = (s32[]{:T(128)}, f32[64,2048]{1,0:T(8,128)S(1)}, bf16[31,64,2048]{2,1,0:T(8,128)(2,1)}, f32[31,64]{1,0:T(8,128)S(1)}, pred[31,64]{1,0:T(8,128)(4,1)S...) while((s32[]{:T(128)}, f32[64,2048]{1,0:T(8,128)S(1)}, ...), condition=%wide.region_5.6_spmd, body=%wide.region_2.0_spmd.sunk | while | flops 4295753728 | bytes 79694160 | solution.py:33
  1662.9 26.0 all-gather.2.cloned.1.call-done
  2419.7 2180.8 %while.32 = (s32[]{:T(128)}, f32[64,2048]{1,0:T(8,128)S(1)}, bf16[30,64,2048]{2,1,0:T(8,128)(2,1)}, pred[30,64]{1,0:T(8,128)(4,1)S(1)}, bf16[30,64,2048]{2,1,0:T...) while((s32[]{:T(128)}, f32[64,2048]{1,0:T(8,128)S(1)}, ...), condition=%wide.region_9.10_spmd.clone, body=%wide.region_7.9_spmd.clone.sunk | while | flops 4296671232 | bytes 88344504 | solution.py:43
  2419.7 28.8 fusion.39
  2450.2 42.5 reduce-scatter.2.cloned.1.call-done
  2494.1 28.7 fusion.39
  2524.6 40.8 reduce-scatter.2.cloned.1.call-done
  2566.7 28.7 fusion.39
  2597.2 40.8 reduce-scatter.2.cloned.1.call-done
  2639.3 28.8 fusion.39
  2669.8 40.8 reduce-scatter.2.cloned.1.call-done
  2711.9 28.7 fusion.39
  2742.5 40.8 reduce-scatter.2.cloned.1.call-done
  2784.6 28.7 fusion.39
  2815.1 40.8 reduce-scatter.2.cloned.1.call-done
  2857.2 28.7 fusion.39
  2887.7 40.8 reduce-scatter.2.cloned.1.call-done
  2929.8 28.7 fusion.39
  2960.4 40.8 reduce-scatter.2.cloned.1.call-done
  3002.4 28.7 fusion.39
  3033.0 40.8 reduce-scatter.2.cloned.1.call-done
  3075.0 28.7 fusion.39
  3105.6 40.8 reduce-scatter.2.cloned.1.call-done
  3147.7 28.8 fusion.39
  3178.2 40.8 reduce-scatter.2.cloned.1.call-done
  3220.3 28.7 fusion.39
  3250.8 40.8 reduce-scatter.2.cloned.1.call-done
  3292.9 28.7 fusion.39
  3323.5 40.9 reduce-scatter.2.cloned.1.call-done
  3365.6 28.8 fusion.39
  3396.2 40.8 reduce-scatter.2.cloned.1.call-done
  3438.3 28.8 fusion.39
  3468.8 40.9 reduce-scatter.2.cloned.1.call-done
  3510.9 28.7 fusion.39
  3541.5 40.8 reduce-scatter.2.cloned.1.call-done
  3583.6 28.7 fusion.39
  3614.1 40.8 reduce-scatter.2.cloned.1.call-done
  3656.2 28.7 fusion.39
  3686.8 40.8 reduce-scatter.2.cloned.1.call-done
  3728.9 28.7 fusion.39
  3759.4 40.8 reduce-scatter.2.cloned.1.call-done
  3801.5 28.8 fusion.39
  3832.1 40.8 reduce-scatter.2.cloned.1.call-done
  3874.2 28.8 fusion.39
  3904.7 40.8 reduce-scatter.2.cloned.1.call-done
  3946.8 28.8 fusion.39
  3977.4 40.8 reduce-scatter.2.cloned.1.call-done
  4019.5 28.7 fusion.39
  4050.0 40.8 reduce-scatter.2.cloned.1.call-done
  4092.1 28.7 fusion.39
  4122.7 40.8 reduce-scatter.2.cloned.1.call-done
  4164.7 28.7 fusion.39
  4195.3 40.8 reduce-scatter.2.cloned.1.call-done
  4237.4 28.7 fusion.39
  4267.9 40.8 reduce-scatter.2.cloned.1.call-done
  4310.0 28.7 fusion.39
  4340.6 40.8 reduce-scatter.2.cloned.1.call-done
  4382.6 28.7 fusion.39
  4413.2 40.8 reduce-scatter.2.cloned.1.call-done
  4455.3 28.7 fusion.39
  4485.8 40.8 reduce-scatter.2.cloned.1.call-done
  4527.9 28.7 fusion.39
  4558.5 40.8 reduce-scatter.2.cloned.1.call-done
  (490 shorter events, 2468.7 us)
Async XLA Ops:
  8.0 47.9 %copy-start.1 = (s32[64,32]{0,1:T(8,128)S(1)}, s32[64,32]{0,1:T(8,128)}, u32[]{:S(2)}) copy-start(s32[64,32]{0,1:T(8,128)} %param.12) | copy-start | bytes 24580
  55.9 34.9 copy-start.3
  99.2 26.0 all-gather.2.cloned.1.call-start
  172.9 26.9 all-gather.2.cloned.1.call-start
  247.5 26.9 all-gather.2.cloned.1.call-start
  322.1 26.6 all-gather.2.cloned.1.call-start
  396.4 26.6 all-gather.2.cloned.1.call-start
  470.7 26.6 all-gather.2.cloned.1.call-start
  545.1 26.9 all-gather.2.cloned.1.call-start
  619.7 26.9 all-gather.2.cloned.1.call-start
  694.3 26.9 all-gather.2.cloned.1.call-start
  768.9 26.6 all-gather.2.cloned.1.call-start
  843.2 26.9 all-gather.2.cloned.1.call-start
  917.9 26.6 all-gather.2.cloned.1.call-start
  992.2 26.9 all-gather.2.cloned.1.call-start
  1066.8 26.6 all-gather.2.cloned.1.call-start
  1141.1 26.6 all-gather.2.cloned.1.call-start
  1215.4 26.6 all-gather.2.cloned.1.call-start
  1289.8 26.6 all-gather.2.cloned.1.call-start
  1364.1 26.6 all-gather.2.cloned.1.call-start
  1438.4 26.9 all-gather.2.cloned.1.call-start
  1513.0 26.6 all-gather.2.cloned.1.call-start
  1587.3 26.9 all-gather.2.cloned.1.call-start
  1661.9 26.9 all-gather.2.cloned.1.call-start
  1736.6 26.9 all-gather.2.cloned.1.call-start
  1811.2 26.6 all-gather.2.cloned.1.call-start
  1885.5 26.9 all-gather.2.cloned.1.call-start
  1960.1 26.6 all-gather.2.cloned.1.call-start
  2034.4 26.6 all-gather.2.cloned.1.call-start
  2108.8 26.9 all-gather.2.cloned.1.call-start
  2183.4 26.9 all-gather.2.cloned.1.call-start
  2258.0 26.6 all-gather.2.cloned.1.call-start
  2332.3 26.9 all-gather.2.cloned.1.call-start
  2406.9 12.7 copy-start
  2419.7 73.1 %reduce-scatter.2.cloned.1.call-start = ((), (), s32[]{:S(2)}) async-start(), calls=%async_computation.2 | async-start | bytes 4718592 | tf_op jit(solution)/shard_map/while/body/eval_jaxpr/reduce_scatter | solution.py:40
  2494.0 71.5 %reduce-scatter.2.cloned.1.call-start = ((), (), s32[]{:S(2)}) async-start(), calls=%async_computation.2 | async-start | bytes 4718592 | tf_op jit(solution)/shard_map/while/body/eval_jaxpr/reduce_scatter | solution.py:40
  2566.6 71.5 %reduce-scatter.2.cloned.1.call-start = ((), (), s32[]{:S(2)}) async-start(), calls=%async_computation.2 | async-start | bytes 4718592 | tf_op jit(solution)/shard_map/while/body/eval_jaxpr/reduce_scatter | solution.py:40
  2639.2 71.5 %reduce-scatter.2.cloned.1.call-start = ((), (), s32[]{:S(2)}) async-start(), calls=%async_computation.2 | async-start | bytes 4718592 | tf_op jit(solution)/shard_map/while/body/eval_jaxpr/reduce_scatter | solution.py:40
  2711.8 71.5 %reduce-scatter.2.cloned.1.call-start = ((), (), s32[]{:S(2)}) async-start(), calls=%async_computation.2 | async-start | bytes 4718592 | tf_op jit(solution)/shard_map/while/body/eval_jaxpr/reduce_scatter | solution.py:40
  2784.5 71.5 %reduce-scatter.2.cloned.1.call-start = ((), (), s32[]{:S(2)}) async-start(), calls=%async_computation.2 | async-start | bytes 4718592 | tf_op jit(solution)/shard_map/while/body/eval_jaxpr/reduce_scatter | solution.py:40
  2857.1 71.5 %reduce-scatter.2.cloned.1.call-start = ((), (), s32[]{:S(2)}) async-start(), calls=%async_computation.2 | async-start | bytes 4718592 | tf_op jit(solution)/shard_map/while/body/eval_jaxpr/reduce_scatter | solution.py:40
  2929.7 71.5 %reduce-scatter.2.cloned.1.call-start = ((), (), s32[]{:S(2)}) async-start(), calls=%async_computation.2 | async-start | bytes 4718592 | tf_op jit(solution)/shard_map/while/body/eval_jaxpr/reduce_scatter | solution.py:40
  3002.3 71.5 %reduce-scatter.2.cloned.1.call-start = ((), (), s32[]{:S(2)}) async-start(), calls=%async_computation.2 | async-start | bytes 4718592 | tf_op jit(solution)/shard_map/while/body/eval_jaxpr/reduce_scatter | solution.py:40
  3074.9 71.5 %reduce-scatter.2.cloned.1.call-start = ((), (), s32[]{:S(2)}) async-start(), calls=%async_computation.2 | async-start | bytes 4718592 | tf_op jit(solution)/shard_map/while/body/eval_jaxpr/reduce_scatter | solution.py:40
  3147.6 71.5 %reduce-scatter.2.cloned.1.call-start = ((), (), s32[]{:S(2)}) async-start(), calls=%async_computation.2 | async-start | bytes 4718592 | tf_op jit(solution)/shard_map/while/body/eval_jaxpr/reduce_scatter | solution.py:40
  3220.2 71.5 %reduce-scatter.2.cloned.1.call-start = ((), (), s32[]{:S(2)}) async-start(), calls=%async_computation.2 | async-start | bytes 4718592 | tf_op jit(solution)/shard_map/while/body/eval_jaxpr/reduce_scatter | solution.py:40
  3292.9 71.5 %reduce-scatter.2.cloned.1.call-start = ((), (), s32[]{:S(2)}) async-start(), calls=%async_computation.2 | async-start | bytes 4718592 | tf_op jit(solution)/shard_map/while/body/eval_jaxpr/reduce_scatter | solution.py:40
  3365.5 71.5 %reduce-scatter.2.cloned.1.call-start = ((), (), s32[]{:S(2)}) async-start(), calls=%async_computation.2 | async-start | bytes 4718592 | tf_op jit(solution)/shard_map/while/body/eval_jaxpr/reduce_scatter | solution.py:40
  3438.2 71.5 %reduce-scatter.2.cloned.1.call-start = ((), (), s32[]{:S(2)}) async-start(), calls=%async_computation.2 | async-start | bytes 4718592 | tf_op jit(solution)/shard_map/while/body/eval_jaxpr/reduce_scatter | solution.py:40
  3510.8 71.5 %reduce-scatter.2.cloned.1.call-start = ((), (), s32[]{:S(2)}) async-start(), calls=%async_computation.2 | async-start | bytes 4718592 | tf_op jit(solution)/shard_map/while/body/eval_jaxpr/reduce_scatter | solution.py:40
  3583.5 71.5 %reduce-scatter.2.cloned.1.call-start = ((), (), s32[]{:S(2)}) async-start(), calls=%async_computation.2 | async-start | bytes 4718592 | tf_op jit(solution)/shard_map/while/body/eval_jaxpr/reduce_scatter | solution.py:40
  3656.1 71.5 %reduce-scatter.2.cloned.1.call-start = ((), (), s32[]{:S(2)}) async-start(), calls=%async_computation.2 | async-start | bytes 4718592 | tf_op jit(solution)/shard_map/while/body/eval_jaxpr/reduce_scatter | solution.py:40
  3728.8 71.5 %reduce-scatter.2.cloned.1.call-start = ((), (), s32[]{:S(2)}) async-start(), calls=%async_computation.2 | async-start | bytes 4718592 | tf_op jit(solution)/shard_map/while/body/eval_jaxpr/reduce_scatter | solution.py:40
  3801.4 71.5 %reduce-scatter.2.cloned.1.call-start = ((), (), s32[]{:S(2)}) async-start(), calls=%async_computation.2 | async-start | bytes 4718592 | tf_op jit(solution)/shard_map/while/body/eval_jaxpr/reduce_scatter | solution.py:40
  3874.1 71.5 %reduce-scatter.2.cloned.1.call-start = ((), (), s32[]{:S(2)}) async-start(), calls=%async_computation.2 | async-start | bytes 4718592 | tf_op jit(solution)/shard_map/while/body/eval_jaxpr/reduce_scatter | solution.py:40
  3946.7 71.5 %reduce-scatter.2.cloned.1.call-start = ((), (), s32[]{:S(2)}) async-start(), calls=%async_computation.2 | async-start | bytes 4718592 | tf_op jit(solution)/shard_map/while/body/eval_jaxpr/reduce_scatter | solution.py:40
  4019.4 71.5 %reduce-scatter.2.cloned.1.call-start = ((), (), s32[]{:S(2)}) async-start(), calls=%async_computation.2 | async-start | bytes 4718592 | tf_op jit(solution)/shard_map/while/body/eval_jaxpr/reduce_scatter | solution.py:40
  4092.0 71.5 %reduce-scatter.2.cloned.1.call-start = ((), (), s32[]{:S(2)}) async-start(), calls=%async_computation.2 | async-start | bytes 4718592 | tf_op jit(solution)/shard_map/while/body/eval_jaxpr/reduce_scatter | solution.py:40
  4164.6 71.5 %reduce-scatter.2.cloned.1.call-start = ((), (), s32[]{:S(2)}) async-start(), calls=%async_computation.2 | async-start | bytes 4718592 | tf_op jit(solution)/shard_map/while/body/eval_jaxpr/reduce_scatter | solution.py:40
  4237.3 71.5 %reduce-scatter.2.cloned.1.call-start = ((), (), s32[]{:S(2)}) async-start(), calls=%async_computation.2 | async-start | bytes 4718592 | tf_op jit(solution)/shard_map/while/body/eval_jaxpr/reduce_scatter | solution.py:40
  4309.9 71.5 %reduce-scatter.2.cloned.1.call-start = ((), (), s32[]{:S(2)}) async-start(), calls=%async_computation.2 | async-start | bytes 4718592 | tf_op jit(solution)/shard_map/while/body/eval_jaxpr/reduce_scatter | solution.py:40
  4382.5 71.5 %reduce-scatter.2.cloned.1.call-start = ((), (), s32[]{:S(2)}) async-start(), calls=%async_computation.2 | async-start | bytes 4718592 | tf_op jit(solution)/shard_map/while/body/eval_jaxpr/reduce_scatter | solution.py:40
  4455.2 71.5 %reduce-scatter.2.cloned.1.call-start = ((), (), s32[]{:S(2)}) async-start(), calls=%async_computation.2 | async-start | bytes 4718592 | tf_op jit(solution)/shard_map/while/body/eval_jaxpr/reduce_scatter | solution.py:40
  4527.8 71.5 %reduce-scatter.2.cloned.1.call-start = ((), (), s32[]{:S(2)}) async-start(), calls=%async_computation.2 | async-start | bytes 4718592 | tf_op jit(solution)/shard_map/while/body/eval_jaxpr/reduce_scatter | solution.py:40
  (1 other events, 7.5 us)
Sparse Core Ops, SparseCore 0:
  102.4 22.7 all-gather.1
  176.1 23.6 all-gather.1
  250.7 23.6 all-gather.1
  325.0 23.6 all-gather.1
  399.3 23.6 all-gather.1
  473.7 23.6 all-gather.1
  548.3 23.6 all-gather.1
  622.9 23.6 all-gather.1
  697.5 23.6 all-gather.1
  771.8 23.6 all-gather.1
  846.5 23.6 all-gather.1
  920.8 23.6 all-gather.1
  995.4 23.6 all-gather.1
  1069.7 23.6 all-gather.1
  1144.0 23.6 all-gather.1
  1218.3 23.6 all-gather.1
  1292.7 23.6 all-gather.1
  1367.0 23.6 all-gather.1
  1441.6 23.6 all-gather.1
  1515.9 23.6 all-gather.1
  1590.5 23.6 all-gather.1
  1665.2 23.6 all-gather.1
  1739.8 23.6 all-gather.1
  1814.1 23.6 all-gather.1
  1888.7 23.6 all-gather.1
  1963.0 23.6 all-gather.1
  2037.4 23.6 all-gather.1
  2112.0 23.6 all-gather.1
  2186.6 23.6 all-gather.1
  2260.9 23.6 all-gather.1
  2335.5 23.6 all-gather.1
  2448.6 44.1 reduce-scatter.1
  2522.9 42.4 reduce-scatter.1
  2595.6 42.4 reduce-scatter.1
  2668.2 42.4 reduce-scatter.1
  2740.8 42.4 reduce-scatter.1
  2813.4 42.4 reduce-scatter.1
  2886.1 42.4 reduce-scatter.1
  2958.7 42.4 reduce-scatter.1
  3031.3 42.4 reduce-scatter.1
  3103.9 42.4 reduce-scatter.1
  3176.6 42.4 reduce-scatter.1
  3249.2 42.4 reduce-scatter.1
  3321.8 42.4 reduce-scatter.1
  3394.5 42.4 reduce-scatter.1
  3467.2 42.4 reduce-scatter.1
  3539.8 42.4 reduce-scatter.1
  3612.5 42.4 reduce-scatter.1
  3685.1 42.4 reduce-scatter.1
  3757.8 42.4 reduce-scatter.1
  3830.4 42.4 reduce-scatter.1
  3903.0 42.4 reduce-scatter.1
  3975.7 42.4 reduce-scatter.1
  4048.4 42.4 reduce-scatter.1
  4121.0 42.4 reduce-scatter.1
  4193.6 42.4 reduce-scatter.1
  4266.3 42.4 reduce-scatter.1
  4338.9 42.4 reduce-scatter.1
  4411.5 42.4 reduce-scatter.1
  4484.2 42.4 reduce-scatter.1
  4556.8 42.4 reduce-scatter.1
where the time goes:
time: 4660 us; the launch traced here: 4650 us
  waiting for transfers between devices  2030 us (44%)
  matrix products  1690 us (36%)
  blocking collectives  715 us (15%)
  other arithmetic  130 us (3%)
  local copies, waits for them, and re-layouts  69.8 us (1%)
    reduce_scatter x30, waiting for transfers between devices, backward_step(): lax.psum_scatter(partial_sum, 'states', scatter_dimension=1, tiled=True)  1230 us
    dot_general x30, matrix products, backward_step(): lax.dot_general(weight, trans_loc, (((1,), (1,)), ((), ())), preferred_el...  862 us
    all_gather x31, waiting for transfers between devices, forward_step(): alpha_full = lax.all_gather(alpha_bf, 'states', axis=1, tiled=True)  800 us
    dot_general x31, matrix products, forward_step(): jnp.dot(alpha_full, trans_loc, preferred_element_type=jnp.float32)  782 us
    psum x31, blocking collectives, forward_step(): norm_sum = lax.psum(jnp.sum(new_mass, axis=1), 'states')  690 us
  transfers between devices with their start and end apart: 61, of which 61 were waited for; matrix products, arithmetic and copies ran while one was open for 1% of the time, Pallas kernels for 0%

commit v1 on v0

v1 whole, which is shorter than its diff:
```python
import functools

import jax
import jax.numpy as jnp
from jax import lax
from jax.experimental import pallas as pl
from jax.experimental.pallas import tpu as pltpu
from jax.sharding import PartitionSpec as P

MESH = pl.DeviceIdType.MESH
LANES = 128
TOP = 2.0 ** 90
SLOT = {'P': 0, 'R2': 1, 'R1p': 2, 'R2p': 3, 'D': 4, 'Dp': 5, 'R1': 5, 'O': 5}
SHARED = 5


def run_kernel(steps, seqs, block, trans, emit, init, lens, post, stats_c, stats_g, hist, vout,
               res, full, wq, acc, ef, eb, psend, pown, qbuf, rbuf, vbuf, gcol, msgc, msgg,
               res_sem, shared_sem, e_sem, h_sem, csend, crecv, gsend, grecv,
               ag_send, ag_recv, ps_send, q_recv, q_send, r_recv):
    me = lax.axis_index('states')
    core = lax.rem(me, 2)
    xpos = lax.rem(lax.div(me, 2), 2)
    ypos = lax.div(me, 4)
    xn = me + 2 - 4 * xpos
    yn = me + 4 - 8 * ypos
    flip = 1 - 2 * core
    r1 = xn + core * (yn - xn)
    r2 = yn + core * (xn - yn)
    dg = xn + yn - me
    dev = {'O': me, 'P': me + flip, 'R1': r1, 'R1p': r1 + flip, 'R2': r2, 'R2p': r2 + flip, 'D': dg, 'Dp': dg + flip}
    others = ['P', 'R1', 'R2', 'R1p', 'R2p', 'D', 'Dp']
    chunks = [pl.ds(c * LANES, LANES) for c in range(block // LANES)]
    tile = min(1024, block)
    half = block // 2

    def remote(src, dst, send, recv, target):
        return pltpu.make_async_remote_copy(src_ref=src, dst_ref=dst, send_sem=send, recv_sem=recv,
                                            device_id={'states': target}, device_id_type=MESH)

    barrier = pltpu.get_barrier_semaphore()
    for rel in others:
        pl.semaphore_signal(barrier, inc=1, device_id={'states': dev[rel]}, device_id_type=MESH)
    pl.semaphore_wait(barrier, 7)

    def shared_copies(rel):
        return [pltpu.make_async_copy(trans.at[pl.ds(dev[rel] * block + h * half, half), :],
                                      res.at[SHARED, pl.ds(h * half, half), :], shared_sem.at[h]) for h in range(2)]

    def shared_start(rel):
        for copy in shared_copies(rel):
            copy.start()

    def shared_wait(rel):
        for copy in shared_copies(rel):
            copy.wait()

    def resident(rel):
        return pltpu.make_async_copy(trans.at[pl.ds(dev[rel] * block, block), :], res.at[SLOT[rel]], res_sem.at[SLOT[rel]])

    def emit_f(t):
        return pltpu.make_async_copy(emit.at[t], ef, e_sem.at[0])

    def emit_b(t):
        return pltpu.make_async_copy(emit.at[t], eb, e_sem.at[1])

    def v_out(t):
        return pltpu.make_async_copy(vbuf, vout.at[t - 1], h_sem.at[0])

    def hist_out(k):
        return pltpu.make_async_copy(full.at[me], hist.at[k], h_sem.at[1])

    def msg_copy(buf, send, recv, i):
        return remote(buf.at[me], buf.at[me], send.at[i], recv.at[me], dev[others[i]])

    def msg_arrival(buf, send, recv, i):
        q = dev[others[i]]
        return remote(buf.at[q], buf.at[q], send.at[i], recv.at[q], q)

    def to_row(part, op):
        wide = jnp.concatenate([part] * (LANES // seqs), axis=0)
        return op(jnp.transpose(wide), axis=0, keepdims=True)

    def to_col(row):
        return jnp.transpose(jnp.broadcast_to(row, (LANES, LANES)))[:seqs]

    ag_names = ['O>P', 'O>R1', 'O>R2', 'R1>R2', 'R1>P', 'R2>P', 'D>P']
    lands = {'O>P': 'P', 'O>R1': 'R1', 'O>R2': 'R2', 'R1>R2': 'D', 'R1>P': 'R2p', 'R2>P': 'R1p', 'D>P': 'Dp'}
    ag_index = {'P': 0, 'R1': 1, 'R2': 2, 'D': 3, 'R2p': 4, 'R1p': 5, 'Dp': 6}

    def ag(name):
        what, where = name.split('>')
        src = dev[what]
        return remote(full.at[src], full.at[src], ag_send.at[ag_names.index(name)], ag_recv.at[ag_index[lands[name]]], dev[where])

    def ag_wait(rel):
        src = dev[rel]
        remote(full.at[src], full.at[src], ag_send.at[0], ag_recv.at[ag_index[rel]], src).wait_recv()

    def to_partner(slot):
        return remote(psend, qbuf.at[slot], ps_send, q_recv.at[slot], dev['P'])

    def outward(slot):
        return remote(qbuf.at[slot], rbuf.at[slot], q_send.at[slot], r_recv.at[slot], dev['R2' if slot == 2 else 'R1'])

    def add_to(dst, src):
        for c in chunks:
            dst[:, c] += src[:, c]

    def f_block(rel, first=False):
        @pl.loop(0, block // tile)
        def _(i):
            c = pl.ds(pl.multiple_of(i * tile, tile), tile)
            r = jnp.dot(full[dev[rel]], res[SLOT[rel], :, c], preferred_element_type=jnp.float32)
            if first:
                acc[:, c] = r
            else:
                acc[:, c] += r

    def b_block(rel, dst):
        @pl.loop(0, block // tile)
        def _(i):
            c = pl.ds(pl.multiple_of(i * tile, tile), tile)
            dst[:, c] = lax.dot_general(wq[...], res[SLOT[rel], c, :], (((1,), (1,)), ((), ())), preferred_element_type=jnp.float32)

    def send_norm():
        part = acc[:, chunks[0]]
        for c in chunks[1:]:
            part = part + acc[:, c]
        msgc[me] = jnp.broadcast_to(to_row(part, jnp.sum), (8, LANES))
        for i in range(7):
            msg_copy(msgc, csend, crecv, i).start()

    def take_norm(k):
        for i in range(7):
            msg_arrival(msgc, csend, crecv, i).wait_recv()
        total = msgc[0]
        for d in range(1, 8):
            total = total + msgc[d]
        row = total[0:1]
        stats_c[pl.ds(k, 1), :] = row
        norm = to_col(row)
        live = lens[...] > k
        for c in chunks:
            post[:, c] = jnp.where(live, acc[:, c] / norm, post[:, c])

    shared_start('Dp')
    emit_f(0).start()
    emit_b(steps - 1).start()
    for rel in ('D', 'R2p', 'R1p', 'R2', 'P'):
        resident(rel).start()
    post[...] = jnp.zeros_like(post)
    gcol[...] = jnp.ones_like(gcol)
    stats_g[...] = jnp.ones_like(stats_g)
    qbuf[3] = jnp.zeros((seqs, block), jnp.float32)
    rbuf[1] = jnp.zeros((seqs, block), jnp.float32)
    rbuf[2] = jnp.zeros((seqs, block), jnp.float32)
    emit_f(0).wait()
    for c in chunks:
        acc[:, c] = init[:, c] * ef[:, c].astype(jnp.float32)
    emit_f(1).start()
    shared_wait('Dp')

    @pl.loop(0, steps - 1)
    def _(k):
        t = steps - 1 - k
        both = k < steps - 2

        send_norm()
        take_norm(k)
        for c in chunks:
            full[me, :, c] = post[:, c].astype(jnp.bfloat16)
        for name in ('O>R1', 'O>R2', 'O>P'):
            ag(name).start()
        hist_out(k).start()

        @pl.when(k >= 1)
        def _():
            for slot in range(3):
                outward(slot).wait_send()
            to_partner(3).wait_send()
            remote(rbuf.at[1], rbuf.at[1], q_send.at[1], r_recv.at[1], dev['R1']).wait_recv()
            remote(rbuf.at[2], rbuf.at[2], q_send.at[2], r_recv.at[2], dev['R2']).wait_recv()
            v_out(t + 1).wait()

        emit_b(t).wait()
        live_next = lens[...] > t + 1
        live = lens[...] > t
        rate = TOP / jnp.where(live_next, gcol[...], 1.0)
        dead = jnp.where(live_next, 0.0, 1.0)
        top = jnp.zeros((seqs, LANES), jnp.float32)
        for c in chunks:
            beta = (qbuf[3, :, c] + rbuf[1, :, c]) + rbuf[2, :, c] + dead
            v = eb[:, c].astype(jnp.float32) * beta
            vbuf[:, c] = v
            w = jnp.where(live, v * rate, 0.0)
            top = jnp.maximum(top, w)
            wq[:, c] = w.astype(jnp.bfloat16)
        v_out(t).start()
        emit_b(t - 1).start()

        @pl.when(both)
        def _():
            msgg[me] = jnp.broadcast_to(to_row(top, jnp.max), (8, LANES))
            for i in range(7):
                msg_copy(msgg, gsend, grecv, i).start()
            b_block('Dp', psend)

        shared_start('R1')

        @pl.when(both)
        def _():
            for i in range(7):
                msg_arrival(msgg, gsend, grecv, i).wait_recv()
            peak = msgg[0]
            for d in range(1, 8):
                peak = jnp.maximum(peak, msgg[d])
            stats_g[pl.ds(k, 1), :] = peak[0:1]
            gcol[...] = to_col(peak[0:1])
            to_partner(0).start()

        @pl.when(k == 0)
        def _():
            resident('D').wait()

        @pl.when(both)
        def _():
            b_block('D', pown)
            to_partner(0).wait()
            add_to(qbuf.at[0], pown)
            outward(0).start()

        @pl.when(k == 0)
        def _():
            resident('R2p').wait()

        @pl.when(both)
        def _():
            b_block('R2p', psend)
            to_partner(1).start()

        shared_wait('R1')

        @pl.when(both)
        def _():
            b_block('R1', pown)
            to_partner(1).wait()
            add_to(qbuf.at[1], pown)
            outward(1).start()

        shared_start('O')
        ag_wait('R1')
        ag('R1>R2').start()
        ag('R1>P').start()
        ag_wait('R2')
        ag('R2>P').start()

        @pl.when(k == 0)
        def _():
            for rel in ('R1p', 'R2', 'P'):
                resident(rel).wait()

        @pl.when(both)
        def _():
            b_block('R1p', psend)
            to_partner(2).start()
            b_block('R2', pown)
            to_partner(2).wait()
            add_to(qbuf.at[2], pown)
            b_block('P', psend)
            to_partner(3).start()

        shared_wait('O')

        @pl.when(both)
        def _():
            b_block('O', pown)
            to_partner(3).wait_recv()
            add_to(qbuf.at[3], pown)

        f_block('O', first=True)
        shared_start('R1')
        ag_wait('P')
        f_block('P')

        @pl.when(both)
        def _():
            remote(rbuf.at[0], rbuf.at[0], q_send.at[0], r_recv.at[0], dev['R1']).wait_recv()
            add_to(qbuf.at[2], rbuf.at[0])
            outward(2).start()

        ag_wait('D')
        ag('D>P').start()
        f_block('R2')
        ag_wait('R1p')
        f_block('R1p')
        shared_wait('R1')
        f_block('R1')
        shared_start('Dp')
        ag_wait('R2p')
        f_block('R2p')
        f_block('D')
        ag_wait('Dp')
        shared_wait('Dp')
        f_block('Dp')

        emit_f(k + 1).wait()
        for c in chunks:
            acc[:, c] = acc[:, c] * ef[:, c].astype(jnp.float32)

        @pl.when(k < steps - 2)
        def _():
            emit_f(k + 2).start()

        for name in ag_names:
            ag(name).wait_send()
        hist_out(k).wait()
        for i in range(7):
            msg_copy(msgc, csend, crecv, i).wait_send()

        @pl.when(both)
        def _():
            for i in range(7):
                msg_copy(msgg, gsend, grecv, i).wait_send()

    v_out(1).wait()
    emit_b(0).wait()
    send_norm()
    take_norm(steps - 1)
    for i in range(7):
        msg_copy(msgc, csend, crecv, i).wait_send()


def solution(mesh):
    def local_run(trans_loc, emit_loc, init_loc, tokens_loc, lengths_loc):
        seqs, steps = tokens_loc.shape
        block = trans_loc.shape[1]
        emit_seq = jnp.take(emit_loc, tokens_loc.T, axis=1, mode='clip')
        emit_seq = jnp.transpose(emit_seq, (1, 2, 0))
        lens = jnp.broadcast_to(lengths_loc[:, None], (seqs, LANES))
        f32, bf16 = jnp.float32, jnp.bfloat16
        sd = jax.ShapeDtypeStruct
        vmem = pl.BlockSpec(memory_space=pltpu.VMEM)
        hbm = pl.BlockSpec(memory_space=pl.ANY)
        dma = pltpu.SemaphoreType.DMA
        post, stats_c, stats_g, hist, vout = pl.pallas_call(
            functools.partial(run_kernel, steps, seqs, block),
            out_shape=(sd((seqs, block), f32), sd((steps, LANES), f32), sd((steps, LANES), f32),
                       sd((steps - 1, seqs, block), bf16), sd((steps - 1, seqs, block), f32)),
            in_specs=[hbm, hbm, vmem, vmem],
            out_specs=(vmem, vmem, vmem, hbm, hbm),
            scratch_shapes=[
                pltpu.VMEM((6, block, block), bf16),
                pltpu.VMEM((8, seqs, block), bf16),
                pltpu.VMEM((seqs, block), bf16),
                pltpu.VMEM((seqs, block), f32),
                pltpu.VMEM((seqs, block), bf16),
                pltpu.VMEM((seqs, block), bf16),
                pltpu.VMEM((seqs, block), f32),
                pltpu.VMEM((seqs, block), f32),
                pltpu.VMEM((4, seqs, block), f32),
                pltpu.VMEM((3, seqs, block), f32),
                pltpu.VMEM((seqs, block), f32),
                pltpu.VMEM((seqs, LANES), f32),
                pltpu.VMEM((8, 8, LANES), f32),
                pltpu.VMEM((8, 8, LANES), f32),
                dma((5,)), dma((2,)), dma((2,)), dma((2,)), dma((7,)), dma((8,)), dma((7,)), dma((8,)),
                dma((7,)), dma((7,)), dma, dma((4,)), dma((3,)), dma((3,)),
            ],
            compiler_params=pltpu.CompilerParams(collective_id=0, has_side_effects=True, vmem_limit_bytes=63 * 2 ** 20),
            name='hmm',
        )(trans_loc, emit_seq, init_loc[None, :], lens)

        norm = stats_c[:, :seqs]
        peak = stats_g[:, :seqs]
        log_norm = jnp.log(norm)
        live = jnp.arange(steps)[:, None] < lengths_loc[None, :]
        loglik = jnp.sum(jnp.where(live, log_norm, 0.0), axis=0)
        scales = [None] * steps
        sigma = jnp.ones((seqs,), f32)
        for t in range(steps - 1, 0, -1):
            if t == steps - 1:
                rate = jnp.full((seqs,), TOP, f32)
            else:
                rate = TOP / jnp.where(live[t + 1], peak[steps - 2 - t], 1.0)
            here = sigma / norm[t]
            scales[t] = jnp.where(live[t], here, 0.0)
            sigma = jnp.where(live[t], here / rate, 1.0)
        scale = jnp.stack(scales[1:])
        weights = (vout * scale[:, :, None]).astype(bf16)
        rows = (steps - 1) * seqs
        pair_sum = lax.dot_general(hist.reshape(rows, block), weights.reshape(rows, block), (((0,), (0,)), ((), ())), preferred_element_type=f32)
        diag_block = lax.dynamic_slice_in_dim(trans_loc, lax.axis_index('states') * block, block, axis=0)
        counts = diag_block.astype(f32) * pair_sum
        return loglik, post, counts

    return jax.shard_map(local_run, mesh=mesh, in_specs=(P(None, 'states'), P('states', None), P('states'), P('seqs', None), P('seqs')), out_specs=(P('seqs'), P('seqs', 'states'), P(('seqs', 'states'), None)), check_vma=False)
```

time: 4660 us -> 1510 us (0.32)
  waiting for transfers between devices: 2030 us -> 0 us
  matrix products: 1690 us -> 26 us
  Pallas kernels: 0 us -> 1410 us
  blocking collectives: 715 us -> 0 us
  other arithmetic: 130 us -> 24.6 us
    dot_general x63 -> x1, matrix products: 1690 us -> 26 us  [local_run(): lax.dot_general(hist.reshape(rows, block), weights.reshape(rows, block),...]
    pallas_call x0 -> x1, Pallas kernels: none -> 1410 us  [local_run(): pl.pallas_call(functools.partial(run_kernel, steps, seqs, block), out_sha...]
    reduce_scatter x30 -> x0, waiting for transfers between devices: 1230 us -> none  [backward_step(): lax.psum_scatter(partial_sum, 'states', scatter_dimension=1, tiled=True)]
    all_gather x31 -> x0, waiting for transfers between devices: 800 us -> none  [forward_step(): alpha_full = lax.all_gather(alpha_bf, 'states', axis=1, tiled=True)]
    psum x32 -> x0, blocking collectives: 715 us -> none  [the longest x31 690 us: forward_step(): norm_sum = lax.psum(jnp.sum(new_mass, axis=1), 'states')]
    dynamic_update_slice x61 -> x0, other arithmetic: 80.1 us -> none  [the longest x30 53.5 us: local_run(): lax.scan(backward_step, jnp.ones((seq_count, block_size), jnp.float32), (...]
  transfers between devices with their start and end apart: 61 -> 0, of which waited for: 61 -> 0; matrix products, arithmetic and copies ran while one was open for 1% -> 0% of each run, Pallas kernels for 0% -> 0%
where the time goes in v1:
time: 1510 us
  Pallas kernels  1410 us (93%)
  local copies, waits for them, and re-layouts  51 us (3%)
  matrix products  26 us (2%)
  other arithmetic  24.6 us (2%)
    pallas_call x1, Pallas kernels, local_run(): pl.pallas_call(functools.partial(run_kernel, steps, seqs, block), out_sha...  1410 us
    gather x1, local copies, waits for them, and re-layouts, local_run(): emit_seq = jnp.take(emit_loc, tokens_loc.T, axis=1, mode='clip')  47.9 us

profile of v1, /device:TPU:0, one launch (start us, length us, event | category | flops | bytes accessed | tf_op | source)
XLA Modules:
  0.0 1508.2 jit_solution(17576786593784264333)
XLA Ops:
  0.6 0.7 iota_compare_fusion
  1.3 0.8 reshape.13
  2.1 1.3 broadcast_in_dim.118.lens
  3.4 47.9 %gather_fusion = bf16[2048,2048]{1,0:T(8,128)(2,1)} fusion(bf16[2048,10000]{0,1:T(8,128)(2,1)} %param.6, s32[2048]{0:T(1024)S(1)} %broadcast_clamp_fusion), kind=kCustom, calls=%fused_computation | custom fusion | bytes 16785408 | tf_op jit(solution)/shard_map/jit(_take)/gather | solution.py:338
  51.4 0.0 copy-start.1
  51.4 1405.8 %hmm.1 = (f32[64,2048]{1,0:T(8,128)}, f32[32,128]{1,0:T(8,128)}, f32[32,128]{1,0:T(8,128)}, bf16[31,64,2048]{2,1,0:T(8,128)(2,1)}, f32[31,64,2048]{2,1,0:T(8,128)}) custom-call(bf16[16384,2048]{1,0:T(8,128)(2,1)} %trans.1, bf16[32,64,2048]{2,1,0:T(8,128)(2,1)} %bitcast.6, f32[1,2048]{1,0:T(1,128)} %bitcast.8, s32[64,128]{1,0:T(8,128)} %broadcast_in_dim.118.lens), custom_call_target="tpu_custom_call" | custom-call | tf_op jit(solution)/shard_map/hmm/pallas_call | solution.py:346
  1457.2 0.0 copy-done.1
  1457.2 1.3 select_reduce_fusion
  1458.5 0.7 broadcast_select_fusion
  1459.2 0.8 divide_select_fusion.1
  1459.9 0.8 divide_select_fusion.2
  1460.7 0.8 divide_select_fusion.3
  1461.5 0.8 divide_select_fusion.4
  1462.2 0.8 divide_select_fusion.5
  1463.0 0.8 divide_select_fusion.6
  1463.8 0.7 divide_select_fusion.7
  1464.5 0.8 divide_select_fusion.8
  1465.2 0.8 divide_select_fusion.9
  1466.0 0.8 divide_select_fusion.10
  1466.8 0.8 divide_select_fusion.11
  1467.6 0.8 divide_select_fusion.12
  1468.3 0.8 divide_select_fusion.13
  1469.1 0.8 divide_select_fusion.14
  1469.9 0.7 divide_select_fusion.15
  1470.6 0.8 divide_select_fusion.16
  1471.4 0.8 divide_select_fusion.17
  1472.1 0.8 divide_select_fusion.18
  1472.9 0.8 divide_select_fusion.19
  1473.7 0.8 divide_select_fusion.20
  1474.4 0.8 divide_select_fusion.21
  1475.2 0.8 divide_select_fusion.22
  1475.9 0.7 divide_select_fusion.23
  1476.6 0.8 divide_select_fusion.24
  1477.4 0.8 divide_select_fusion.25
  1478.2 0.8 divide_select_fusion.26
  1479.0 0.8 divide_select_fusion.27
  1479.7 0.8 slice_select_fusion.1
  1480.5 0.8 slice_select_fusion
  1481.3 0.1 stack.2
  1481.4 0.0 copy-start
  1481.4 26.0 %bitcast_multiply_fusion = f32[2048,2048]{1,0:T(8,128)} fusion(bf16[31,64,2048]{2,1,0:T(8,128)(2,1)} %get-tuple-element.10, bf16[16384,2048]{1,0:T(8,128)(2,1)} %trans.1, s32[]{:T(128)S(6)} %select_n.1210, f32[31,64,2048]{2,1,0:T(8,128)} %get-tuple-element.11, f32[31,64]{1,0:T(8,128)S(1)} %stack.2), kind=kOutput, calls=%fused_computation.1 | convolution fusion | flops 16659513344 | bytes 49553156 | tf_op jit(solution)/shard_map/dot_general | solution.py:392
  1507.4 0.0 copy-done
  1507.4 0.8 copy.9
  (1 shorter events, 0.0 us)
Async XLA Ops:
  51.4 1405.9 %copy-start.1 = (s32[64]{0:T(128)S(1)}, s32[64]{0:T(128)}, u32[]{:S(2)}) copy-start(s32[64]{0:T(128)} %param.9) | copy-start | bytes 772
  1481.4 26.0 %copy-start = (f32[64,2048]{1,0:T(8,128)S(1)}, f32[64,2048]{1,0:T(8,128)}, u32[]{:S(2)}) copy-start(f32[64,2048]{1,0:T(8,128)} %get-tuple-element.76) | copy-start | bytes 1572868

commit v2 on v0

v2 whole, which is shorter than its diff:
```python
import functools

import jax
import jax.numpy as jnp
from jax import lax
from jax.experimental import pallas as pl
from jax.experimental.pallas import tpu as pltpu
from jax.sharding import PartitionSpec as P

MESH = pl.DeviceIdType.MESH
LANES = 128
SLOT = {'O': 0, 'R2': 1, 'R2p': 2, 'R1p': 3, 'Dp': 4, 'P': 5, 'R1': 5, 'D': 5}
SHARED = 5
PIECES = 4


def run_kernel(steps, seqs, block, trans, emit, init, lens, post, stats_c, hist, whist,
               res, full, wq, acc, ef, eb, psend, pown, qbuf, rbuf, msgc,
               res_sem, shared_sem, e_sem, h_sem, csend, crecv,
               ag_send, ag_recv, ps_send, q_recv, q_send, r_recv, credit):
    me = lax.axis_index('states')
    core = lax.rem(me, 2)
    xpos = lax.rem(lax.div(me, 2), 2)
    ypos = lax.div(me, 4)
    xn = me + 2 - 4 * xpos
    yn = me + 4 - 8 * ypos
    flip = 1 - 2 * core
    r1 = xn + core * (yn - xn)
    r2 = yn + core * (xn - yn)
    dg = xn + yn - me
    dev = {'O': me, 'P': me + flip, 'R1': r1, 'R1p': r1 + flip, 'R2': r2, 'R2p': r2 + flip, 'D': dg, 'Dp': dg + flip}
    others = ['P', 'R1', 'R2', 'R1p', 'R2p', 'D', 'Dp']
    chunks = [pl.ds(c * LANES, LANES) for c in range(block // LANES)]
    half = block // 2
    halves = [pl.ds(h * half, half) for h in range(2)]
    part = block // PIECES
    parts = [pl.ds(p * part, part) for p in range(PIECES)]
    per_part = [[pl.ds(p * part + c * LANES, LANES) for c in range(max(1, part // LANES))] for p in range(PIECES)]

    def remote(src, dst, send, recv, target):
        return pltpu.make_async_remote_copy(src_ref=src, dst_ref=dst, send_sem=send, recv_sem=recv,
                                            device_id={'states': target}, device_id_type=MESH)

    barrier = pltpu.get_barrier_semaphore()
    for rel in others:
        pl.semaphore_signal(barrier, inc=1, device_id={'states': dev[rel]}, device_id_type=MESH)
    pl.semaphore_wait(barrier, 7)

    def shared(rel, h):
        return pltpu.make_async_copy(trans.at[pl.ds(dev[rel] * block + h * half, half), :],
                                     res.at[SHARED, halves[h], :], shared_sem.at[h])

    def shared_start(rel):
        shared(rel, 0).start()
        shared(rel, 1).start()

    def shared_wait(rel):
        shared(rel, 0).wait()
        shared(rel, 1).wait()

    def resident(rel):
        return pltpu.make_async_copy(trans.at[pl.ds(dev[rel] * block, block), :], res.at[SLOT[rel]], res_sem.at[SLOT[rel]])

    def emit_f(t):
        return pltpu.make_async_copy(emit.at[t], ef, e_sem.at[0])

    def emit_b(t):
        return pltpu.make_async_copy(emit.at[t], eb, e_sem.at[1])

    def whist_out(t):
        return pltpu.make_async_copy(wq, whist.at[t - 1], h_sem.at[0])

    def hist_out(k):
        return pltpu.make_async_copy(full.at[me], hist.at[k], h_sem.at[1])

    def norm_msg(i):
        return remote(msgc.at[me], msgc.at[me], csend.at[i], crecv.at[me], dev[others[i]])

    def norm_arrival(i):
        q = dev[others[i]]
        return remote(msgc.at[q], msgc.at[q], csend.at[i], crecv.at[q], q)

    def grant(i, rel):
        pl.semaphore_signal(credit.at[i], inc=1, device_id={'states': dev[rel]}, device_id_type=MESH)

    def to_row(lanes):
        wide = jnp.concatenate([lanes] * (LANES // seqs), axis=0)
        return jnp.sum(jnp.transpose(wide), axis=0, keepdims=True)

    def to_col(row):
        return jnp.transpose(jnp.broadcast_to(row, (LANES, LANES)))[:seqs]

    ag_names = ['O>P', 'O>R1', 'O>R2', 'R1>R2', 'R1>P', 'R2>P', 'D>P']
    lands = {'O>P': 'P', 'O>R1': 'R1', 'O>R2': 'R2', 'R1>R2': 'D', 'R1>P': 'R2p', 'R2>P': 'R1p', 'D>P': 'Dp'}
    ag_index = {'P': 0, 'R1': 1, 'R2': 2, 'D': 3, 'R2p': 4, 'R1p': 5, 'Dp': 6}

    def ag(name, h):
        what, where = name.split('>')
        place = full.at[dev[what], :, halves[h]]
        return remote(place, place, ag_send.at[ag_names.index(name), h], ag_recv.at[ag_index[lands[name]], h], dev[where])

    def ag_wait(rel, h):
        place = full.at[dev[rel], :, halves[h]]
        remote(place, place, ag_send.at[0, h], ag_recv.at[ag_index[rel], h], dev[rel]).wait_recv()

    def ag_pass(h):
        ag_wait('R1', h)
        ag('R1>R2', h).start()
        ag('R1>P', h).start()
        ag_wait('R2', h)
        ag('R2>P', h).start()

    def to_partner(slot, p):
        return remote(psend.at[:, parts[p]], qbuf.at[slot, :, parts[p]], ps_send.at[p], q_recv.at[slot, p], dev['P'])

    def outward(slot, p):
        return remote(qbuf.at[slot, :, parts[p]], rbuf.at[slot, :, parts[p]], q_send.at[slot, p], r_recv.at[slot, p],
                      dev['R2' if slot == 2 else 'R1'])

    def inward(slot, p):
        place = rbuf.at[slot, :, parts[p]]
        remote(place, place, q_send.at[slot, p], r_recv.at[slot, p], dev['R2' if slot == 2 else 'R1']).wait_recv()

    def f_half(rel, h, first=False):
        r = jnp.dot(full[dev[rel], :, halves[h]], res[SLOT[rel], halves[h], :], preferred_element_type=jnp.float32)
        if first:
            acc[...] = r
        else:
            acc[...] += r

    def b_part(rel, p, dst):
        dst[:, parts[p]] = lax.dot_general(wq[...], res[SLOT[rel], parts[p], :], (((1,), (1,)), ((), ())),
                                           preferred_element_type=jnp.float32)

    def send_norm():
        lanes = acc[:, chunks[0]]
        for c in chunks[1:]:
            lanes = lanes + acc[:, c]
        msgc[me] = jnp.broadcast_to(to_row(lanes), (8, LANES))
        for i in range(7):
            norm_msg(i).start()

    def take_norm(k):
        for i in range(7):
            norm_arrival(i).wait_recv()
        total = msgc[0]
        for d in range(1, 8):
            total = total + msgc[d]
        row = total[0:1]
        stats_c[pl.ds(k, 1), :] = row
        norm = to_col(row)
        live = lens[...] > k
        for c in chunks:
            post[:, c] = jnp.where(live, acc[:, c] / norm, post[:, c])

    def send_alpha():
        for c in chunks:
            full[me, :, c] = post[:, c].astype(jnp.bfloat16)
        for h in range(2):
            for name in ('O>R1', 'O>R2', 'O>P'):
                ag(name, h).start()

    def weigh(t):
        norm = to_col(stats_c[pl.ds(t, 1), :])
        live = lens[...] > t
        dead = jnp.where(lens[...] > t + 1, 0.0, 1.0)
        for c in chunks:
            beta = (qbuf[3, :, c] + rbuf[1, :, c]) + rbuf[2, :, c] + dead
            w = eb[:, c].astype(jnp.float32) * beta / norm
            wq[:, c] = jnp.where(live, w, 0.0).astype(jnp.bfloat16)

    resident('O').start()
    emit_f(0).start()
    emit_b(steps - 1).start()
    shared_start('P')
    for rel in ('R2', 'R2p', 'R1p', 'Dp'):
        resident(rel).start()
    post[...] = jnp.zeros_like(post)
    qbuf[3] = jnp.zeros((seqs, block), jnp.float32)
    rbuf[1] = jnp.zeros((seqs, block), jnp.float32)
    rbuf[2] = jnp.zeros((seqs, block), jnp.float32)
    emit_f(0).wait()
    for c in chunks:
        acc[:, c] = init[:, c] * ef[:, c].astype(jnp.float32)
    emit_f(1).start()
    send_norm()
    take_norm(0)
    send_alpha()
    resident('O').wait()

    @pl.loop(0, steps - 1)
    def _(k):
        more = k < steps - 2
        hist_out(k).start()
        f_half('O', 0, first=True)
        f_half('O', 1)
        ag_wait('P', 0)
        ag_wait('P', 1)
        shared_wait('P')
        f_half('P', 0)
        f_half('P', 1)
        shared_start('R1')

        @pl.when(k == 0)
        def _():
            for rel in ('R2', 'R2p', 'R1p', 'Dp'):
                resident(rel).wait()

        ag_pass(0)
        f_half('R2', 0)
        ag_wait('R2p', 0)
        f_half('R2p', 0)
        ag_wait('R1p', 0)
        f_half('R1p', 0)
        shared_wait('R1')
        f_half('R1', 0)
        ag_pass(1)
        f_half('R1', 1)
        shared_start('D')
        f_half('R2', 1)
        ag_wait('D', 0)
        ag('D>P', 0).start()
        ag_wait('R2p', 1)
        f_half('R2p', 1)
        ag_wait('R1p', 1)
        f_half('R1p', 1)
        ag_wait('Dp', 0)
        f_half('Dp', 0)
        ag_wait('D', 1)
        ag('D>P', 1).start()
        shared_wait('D')
        f_half('D', 0)
        f_half('D', 1)

        @pl.when(more)
        def _():
            shared_start('P')

        emit_f(k + 1).wait()
        ag_wait('Dp', 1)
        f_half('Dp', 1)
        for c in chunks:
            acc[:, c] = acc[:, c] * ef[:, c].astype(jnp.float32)

        for name in ag_names:
            for h in range(2):
                ag(name, h).wait_send()
        hist_out(k).wait()
        for i in range(7):
            norm_msg(i).wait_send()
        send_norm()

        @pl.when(more)
        def _():
            emit_f(k + 2).start()

        take_norm(k + 1)

        @pl.when(more)
        def _():
            send_alpha()

    for i in range(7):
        norm_msg(i).wait_send()

    @pl.loop(0, steps - 2)
    def _(m):
        t = steps - 1 - m
        emit_b(t).wait()

        @pl.when(m >= 1)
        def _():
            whist_out(t + 1).wait()
            for p in range(PIECES):
                for slot in range(3):
                    outward(slot, p).wait_send()
                to_partner(3, p).wait_send()
                inward(1, p)
                inward(2, p)

        weigh(t)
        for i, rel in enumerate(('P', 'R1', 'R2')):
            grant(i, rel)
        whist_out(t).start()
        emit_b(t - 1).start()

        for slot, (far, near) in enumerate((('Dp', 'D'), ('R2p', 'R1'), ('R1p', 'R2'), ('P', 'O'))):
            for kind, p in ((0, 0), (0, 1), (0, 2), (1, 0), (0, 3), (1, 1), (1, 2), (1, 3)):
                if kind == 0:
                    if slot > 0:
                        to_partner(slot - 1, p).wait_send()
                    if slot == 3 and p == 0:
                        shared_wait('P')
                    b_part(far, p, psend)
                    if slot == 0 and p == 0:
                        pl.semaphore_wait(credit.at[0], 1)
                    to_partner(slot, p).start()
                    if slot == 3 and p == PIECES - 1:
                        shared_start('D')
                    continue
                if slot == 0 and p == 0:
                    @pl.when(m >= 1)
                    def _():
                        shared_wait('D')
                if slot == 1 and p == 0:
                    shared_wait('R1')
                b_part(near, p, pown)
                if slot < 2 and p == PIECES - 1:
                    shared_start('R1' if slot == 0 else 'P')
                to_partner(slot, p).wait_recv()
                if slot == 2:
                    inward(0, p)
                for c in per_part[p]:
                    if slot == 2:
                        qbuf[slot, :, c] = (qbuf[slot, :, c] + pown[:, c]) + rbuf[0, :, c]
                    else:
                        qbuf[slot, :, c] += pown[:, c]
                if slot < 3:
                    if p == 0 and slot != 1:
                        pl.semaphore_wait(credit.at[1 if slot == 0 else 2], 1)
                    outward(slot, p).start()

    emit_b(1).wait()
    whist_out(2).wait()
    for p in range(PIECES):
        for slot in range(3):
            outward(slot, p).wait_send()
        to_partner(3, p).wait_send()
        inward(1, p)
        inward(2, p)
    shared_wait('D')
    weigh(1)
    whist_out(1).start()
    whist_out(1).wait()


def solution(mesh):
    def local_run(trans_loc, emit_loc, init_loc, tokens_loc, lengths_loc):
        seqs, steps = tokens_loc.shape
        block = trans_loc.shape[1]
        emit_seq = jnp.take(emit_loc, tokens_loc.T, axis=1, mode='clip')
        emit_seq = jnp.transpose(emit_seq, (1, 2, 0))
        lens = jnp.broadcast_to(lengths_loc[:, None], (seqs, LANES))
        f32, bf16 = jnp.float32, jnp.bfloat16
        sd = jax.ShapeDtypeStruct
        vmem = pl.BlockSpec(memory_space=pltpu.VMEM)
        hbm = pl.BlockSpec(memory_space=pl.ANY)
        dma = pltpu.SemaphoreType.DMA
        post, stats_c, hist, weights = pl.pallas_call(
            functools.partial(run_kernel, steps, seqs, block),
            out_shape=(sd((seqs, block), f32), sd((steps, LANES), f32),
                       sd((steps - 1, seqs, block), bf16), sd((steps - 1, seqs, block), bf16)),
            in_specs=[hbm, hbm, vmem, vmem],
            out_specs=(vmem, vmem, hbm, hbm),
            scratch_shapes=[
                pltpu.VMEM((6, block, block), bf16),
                pltpu.VMEM((8, seqs, block), bf16),
                pltpu.VMEM((seqs, block), bf16),
                pltpu.VMEM((seqs, block), f32),
                pltpu.VMEM((seqs, block), bf16),
                pltpu.VMEM((seqs, block), bf16),
                pltpu.VMEM((seqs, block), f32),
                pltpu.VMEM((seqs, block), f32),
                pltpu.VMEM((4, seqs, block), f32),
                pltpu.VMEM((3, seqs, block), f32),
                pltpu.VMEM((8, 8, LANES), f32),
                dma((5,)), dma((2,)), dma((2,)), dma((2,)), dma((7,)), dma((8,)),
                dma((7, 2)), dma((7, 2)), dma((PIECES,)), dma((4, PIECES)), dma((3, PIECES)), dma((3, PIECES)),
                pltpu.SemaphoreType.REGULAR((3,)),
            ],
            compiler_params=pltpu.CompilerParams(collective_id=0, has_side_effects=True, vmem_limit_bytes=63 * 2 ** 20),
            name='hmm',
        )(trans_loc, emit_seq, init_loc[None, :], lens)

        norm = stats_c[:, :seqs]
        live = jnp.arange(steps)[:, None] < lengths_loc[None, :]
        loglik = jnp.sum(jnp.where(live, jnp.log(norm), 0.0), axis=0)
        rows = (steps - 1) * seqs
        pair_sum = lax.dot_general(hist.reshape(rows, block), weights.reshape(rows, block), (((0,), (0,)), ((), ())), preferred_element_type=f32)
        diag_block = lax.dynamic_slice_in_dim(trans_loc, lax.axis_index('states') * block, block, axis=0)
        counts = diag_block.astype(f32) * pair_sum
        return loglik, post, counts

    return jax.shard_map(local_run, mesh=mesh, in_specs=(P(None, 'states'), P('states', None), P('states'), P('seqs', None), P('seqs')), out_specs=(P('seqs'), P('seqs', 'states'), P(('seqs', 'states'), None)), check_vma=False)
```

time: 4660 us -> 1440 us (0.31)
  waiting for transfers between devices: 2030 us -> 0 us
  matrix products: 1690 us -> 25 us
  Pallas kernels: 0 us -> 1360 us
  blocking collectives: 715 us -> 0 us
  other arithmetic: 130 us -> 1.26 us
    dot_general x63 -> x1, matrix products: 1690 us -> 25 us  [local_run(): lax.dot_general(hist.reshape(rows, block), weights.reshape(rows, block),...]
    pallas_call x0 -> x1, Pallas kernels: none -> 1360 us  [local_run(): pl.pallas_call(functools.partial(run_kernel, steps, seqs, block), out_sha...]
    reduce_scatter x30 -> x0, waiting for transfers between devices: 1230 us -> none  [backward_step(): lax.psum_scatter(partial_sum, 'states', scatter_dimension=1, tiled=True)]
    all_gather x31 -> x0, waiting for transfers between devices: 800 us -> none  [forward_step(): alpha_full = lax.all_gather(alpha_bf, 'states', axis=1, tiled=True)]
    psum x32 -> x0, blocking collectives: 715 us -> none  [the longest x31 690 us: forward_step(): norm_sum = lax.psum(jnp.sum(new_mass, axis=1), 'states')]
    dynamic_update_slice x61 -> x0, other arithmetic: 80.1 us -> none  [the longest x30 53.5 us: local_run(): lax.scan(backward_step, jnp.ones((seq_count, block_size), jnp.float32), (...]
  transfers between devices with their start and end apart: 61 -> 0, of which waited for: 61 -> 0; matrix products, arithmetic and copies ran while one was open for 1% -> 0% of each run, Pallas kernels for 0% -> 0%
where the time goes in v2:
time: 1440 us
  Pallas kernels  1360 us (94%)
  local copies, waits for them, and re-layouts  50.9 us (4%)
  matrix products  25 us (2%)
    pallas_call x1, Pallas kernels, local_run(): pl.pallas_call(functools.partial(run_kernel, steps, seqs, block), out_sha...  1360 us
    gather x1, local copies, waits for them, and re-layouts, local_run(): emit_seq = jnp.take(emit_loc, tokens_loc.T, axis=1, mode='clip')  47.9 us

profile of v2, /device:TPU:0, one launch (start us, length us, event | category | flops | bytes accessed | tf_op | source)
XLA Modules:
  0.0 1437.3 jit_solution(13612126611196698336)
XLA Ops:
  0.6 0.8 reshape.12
  1.4 1.3 broadcast_in_dim.21.lens
  2.8 47.9 %gather_fusion = bf16[2048,2048]{1,0:T(8,128)(2,1)} fusion(bf16[2048,10000]{0,1:T(8,128)(2,1)} %param.6, s32[2048]{0:T(1024)S(1)} %broadcast_clamp_fusion), kind=kCustom, calls=%fused_computation | custom fusion | bytes 16785408 | tf_op jit(solution)/shard_map/jit(_take)/gather | solution.py:341
  50.7 0.0 copy-start.1
  50.7 1359.5 %hmm.1 = (f32[64,2048]{1,0:T(8,128)}, f32[32,128]{1,0:T(8,128)}, bf16[31,64,2048]{2,1,0:T(8,128)(2,1)}, bf16[31,64,2048]{2,1,0:T(8,128)(2,1)}) custom-call(bf16[16384,2048]{1,0:T(8,128)(2,1)} %trans.1, bf16[32,64,2048]{2,1,0:T(8,128)(2,1)} %bitcast.7, f32[1,2048]{1,0:T(1,128)} %bitcast.9, s32[64,128]{1,0:T(8,128)} %broadcast_in_dim.21.lens), custom_call_target="tpu_custom_call" | custom-call | tf_op jit(solution)/shard_map/hmm/pallas_call | solution.py:349
  1410.2 0.0 copy-done.1
  1410.3 1.3 select_reduce_fusion
  1411.5 0.0 copy-start
  1411.5 25.0 %bitcast_multiply_fusion = f32[2048,2048]{1,0:T(8,128)} fusion(bf16[31,64,2048]{2,1,0:T(8,128)(2,1)} %get-tuple-element.9, bf16[31,64,2048]{2,1,0:T(8,128)(2,1)} %get-tuple-element.10, bf16[16384,2048]{1,0:T(8,128)(2,1)} %trans.1, s32[]{:T(128)S(6)} %select_n.8), kind=kOutput, calls=%fused_computation.1 | convolution fusion | flops 16651386880 | bytes 41418756 | tf_op jit(solution)/shard_map/dot_general | solution.py:379
  1436.5 0.0 copy-done
  1436.5 0.8 copy.9
  (1 shorter events, 0.0 us)
Async XLA Ops:
  50.7 1359.5 %copy-start.1 = (s32[64]{0:T(128)S(1)}, s32[64]{0:T(128)}, u32[]{:S(2)}) copy-start(s32[64]{0:T(128)} %param.9) | copy-start | bytes 772
  1411.5 25.0 %copy-start = (f32[64,2048]{1,0:T(8,128)S(1)}, f32[64,2048]{1,0:T(8,128)}, u32[]{:S(2)}) copy-start(f32[64,2048]{1,0:T(8,128)} %get-tuple-element.15) | copy-start | bytes 1572868

commit v3 on v2

--- a/solution.py
+++ b/solution.py
@@ -33,6 +33,7 @@
     chunks = [pl.ds(c * LANES, LANES) for c in range(block // LANES)]
     half = block // 2
     halves = [pl.ds(h * half, half) for h in range(2)]
+    cuts = [pl.ds(0, half), pl.ds(half, half // 2), pl.ds(half + half // 2, half // 2)]
     part = block // PIECES
     parts = [pl.ds(p * part, part) for p in range(PIECES)]
     per_part = [[pl.ds(p * part + c * LANES, LANES) for c in range(max(1, part // LANES))] for p in range(PIECES)]
@@ -96,11 +97,11 @@
 
     def ag(name, h):
         what, where = name.split('>')
-        place = full.at[dev[what], :, halves[h]]
+        place = full.at[dev[what], :, cuts[h]]
         return remote(place, place, ag_send.at[ag_names.index(name), h], ag_recv.at[ag_index[lands[name]], h], dev[where])
 
     def ag_wait(rel, h):
-        place = full.at[dev[rel], :, halves[h]]
+        place = full.at[dev[rel], :, cuts[h]]
         remote(place, place, ag_send.at[0, h], ag_recv.at[ag_index[rel], h], dev[rel]).wait_recv()
 
     def ag_pass(h):
@@ -121,8 +122,8 @@
         place = rbuf.at[slot, :, parts[p]]
         remote(place, place, q_send.at[slot, p], r_recv.at[slot, p], dev['R2' if slot == 2 else 'R1']).wait_recv()
 
-    def f_half(rel, h, first=False):
-        r = jnp.dot(full[dev[rel], :, halves[h]], res[SLOT[rel], halves[h], :], preferred_element_type=jnp.float32)
+    def f_half(rel, h, first=False, spans=halves):
+        r = jnp.dot(full[dev[rel], :, spans[h]], res[SLOT[rel], spans[h], :], preferred_element_type=jnp.float32)
         if first:
             acc[...] = r
         else:
@@ -154,9 +155,9 @@
             post[:, c] = jnp.where(live, acc[:, c] / norm, post[:, c])
 
     def send_alpha():
-        for c in chunks:
-            full[me, :, c] = post[:, c].astype(jnp.bfloat16)
-        for h in range(2):
+        for h in range(3):
+            for c in chunks[(0, 4, 6)[h] * len(chunks) // 8:(4, 6, 8)[h] * len(chunks) // 8]:
+                full[me, :, c] = post[:, c].astype(jnp.bfloat16)
             for name in ('O>R1', 'O>R2', 'O>P'):
                 ag(name, h).start()
 
@@ -194,8 +195,8 @@
         hist_out(k).start()
         f_half('O', 0, first=True)
         f_half('O', 1)
-        ag_wait('P', 0)
-        ag_wait('P', 1)
+        for h in range(3):
+            ag_wait('P', h)
         shared_wait('P')
         f_half('P', 0)
         f_half('P', 1)
@@ -210,24 +211,29 @@
         f_half('R2', 0)
         ag_wait('R2p', 0)
         f_half('R2p', 0)
+        ag_pass(1)
         ag_wait('R1p', 0)
         f_half('R1p', 0)
         shared_wait('R1')
         f_half('R1', 0)
-        ag_pass(1)
+        ag_pass(2)
         f_half('R1', 1)
         shared_start('D')
         f_half('R2', 1)
         ag_wait('D', 0)
         ag('D>P', 0).start()
         ag_wait('R2p', 1)
+        ag_wait('R2p', 2)
         f_half('R2p', 1)
+        ag_wait('D', 1)
+        ag('D>P', 1).start()
         ag_wait('R1p', 1)
+        ag_wait('R1p', 2)
         f_half('R1p', 1)
+        ag_wait('D', 2)
+        ag('D>P', 2).start()
         ag_wait('Dp', 0)
         f_half('Dp', 0)
-        ag_wait('D', 1)
-        ag('D>P', 1).start()
         shared_wait('D')
         f_half('D', 0)
         f_half('D', 1)
@@ -238,12 +244,14 @@
 
         emit_f(k + 1).wait()
         ag_wait('Dp', 1)
-        f_half('Dp', 1)
+        f_half('Dp', 1, spans=cuts)
+        ag_wait('Dp', 2)
+        f_half('Dp', 2, spans=cuts)
         for c in chunks:
             acc[:, c] = acc[:, c] * ef[:, c].astype(jnp.float32)
 
         for name in ag_names:
-            for h in range(2):
+            for h in range(3):
                 ag(name, h).wait_send()
         hist_out(k).wait()
         for i in range(7):
@@ -365,7 +373,7 @@
                 pltpu.VMEM((3, seqs, block), f32),
                 pltpu.VMEM((8, 8, LANES), f32),
                 dma((5,)), dma((2,)), dma((2,)), dma((2,)), dma((7,)), dma((8,)),
-                dma((7, 2)), dma((7, 2)), dma((PIECES,)), dma((4, PIECES)), dma((3, PIECES)), dma((3, PIECES)),
+                dma((7, 3)), dma((7, 3)), dma((PIECES,)), dma((4, PIECES)), dma((3, PIECES)), dma((3, PIECES)),
                 pltpu.SemaphoreType.REGULAR((3,)),
             ],
             compiler_params=pltpu.CompilerParams(collective_id=0, has_side_effects=True, vmem_limit_bytes=63 * 2 ** 20),

time: 1440 us -> 1440 us (level)
  no operation moved by 1% of the time
where the time goes in v3:
time: 1440 us
  Pallas kernels  1360 us (94%)
  local copies, waits for them, and re-layouts  50.9 us (4%)
  matrix products  25 us (2%)
    pallas_call x1, Pallas kernels, local_run(): pl.pallas_call(functools.partial(run_kernel, steps, seqs, block), out_sha...  1360 us
    gather x1, local copies, waits for them, and re-layouts, local_run(): emit_seq = jnp.take(emit_loc, tokens_loc.T, axis=1, mode='clip')  47.9 us

profile of v3, /device:TPU:0, one launch (start us, length us, event | category | flops | bytes accessed | tf_op | source)
XLA Modules:
  0.0 1437.7 jit_solution(12082962785040761204)
XLA Ops:
  0.6 0.8 reshape.12
  1.4 1.3 broadcast_in_dim.21.lens
  2.8 47.9 %gather_fusion = bf16[2048,2048]{1,0:T(8,128)(2,1)} fusion(bf16[2048,10000]{0,1:T(8,128)(2,1)} %param.6, s32[2048]{0:T(1024)S(1)} %broadcast_clamp_fusion), kind=kCustom, calls=%fused_computation | custom fusion | bytes 16785408 | tf_op jit(solution)/shard_map/jit(_take)/gather | solution.py:349
  50.7 0.0 copy-start.1
  50.7 1359.9 %hmm.1 = (f32[64,2048]{1,0:T(8,128)}, f32[32,128]{1,0:T(8,128)}, bf16[31,64,2048]{2,1,0:T(8,128)(2,1)}, bf16[31,64,2048]{2,1,0:T(8,128)(2,1)}) custom-call(bf16[16384,2048]{1,0:T(8,128)(2,1)} %trans.1, bf16[32,64,2048]{2,1,0:T(8,128)(2,1)} %bitcast.7, f32[1,2048]{1,0:T(1,128)} %bitcast.9, s32[64,128]{1,0:T(8,128)} %broadcast_in_dim.21.lens), custom_call_target="tpu_custom_call" | custom-call | tf_op jit(solution)/shard_map/hmm/pallas_call | solution.py:357
  1410.6 0.0 copy-done.1
  1410.6 1.3 select_reduce_fusion
  1411.9 0.0 copy-start
  1411.9 25.0 %bitcast_multiply_fusion = f32[2048,2048]{1,0:T(8,128)} fusion(bf16[31,64,2048]{2,1,0:T(8,128)(2,1)} %get-tuple-element.9, bf16[31,64,2048]{2,1,0:T(8,128)(2,1)} %get-tuple-element.10, bf16[16384,2048]{1,0:T(8,128)(2,1)} %trans.1, s32[]{:T(128)S(6)} %select_n.8), kind=kOutput, calls=%fused_computation.1 | convolution fusion | flops 16651386880 | bytes 41418756 | tf_op jit(solution)/shard_map/dot_general | solution.py:387
  1436.9 0.0 copy-done
  1436.9 0.8 copy.9
  (1 shorter events, 0.0 us)
Async XLA Ops:
  50.7 1359.9 %copy-start.1 = (s32[64]{0:T(128)S(1)}, s32[64]{0:T(128)}, u32[]{:S(2)}) copy-start(s32[64]{0:T(128)} %param.9) | copy-start | bytes 772
  1411.9 25.0 %copy-start = (f32[64,2048]{1,0:T(8,128)S(1)}, f32[64,2048]{1,0:T(8,128)}, u32[]{:S(2)}) copy-start(f32[64,2048]{1,0:T(8,128)} %get-tuple-element.15) | copy-start | bytes 1572868
